TPU v7x, 32 devices: a whole 2x2x4 slice. The times are simulated.
32 devices in a mesh: fsdp: 4 (over y, x), tenant: 4 (over z), dp: 2 (over core).
Axes of the slice: x: 2, y: 2, z: 4, core: 2. Of those that a mesh axis runs over, the one named last changes fastest.
Arguments:
- tokens: bfloat16 [3072, 5120], P(('fsdp', 'dp'), 'tenant'), may hold values from -6 to 6
- block_tenant_index: int32 [48], P(('fsdp', 'dp')), may hold values from 0 to 7
- ranks: int32 [8], replicated, may hold values from 16 to 64, as said below
- frozen_up_weight: bfloat16 [5120, 14336], P(('fsdp', 'dp'), 'tenant'), may hold values from -0.078125 to 0.078125
- tenant_down_adapters: bfloat16 [8, 64, 5120], P('tenant'), may hold values from -0.078125 to 0.078125
- tenant_up_adapters: bfloat16 [8, 64, 14336], P('tenant'), may hold values from -0.75 to 0.75
- cotangent: bfloat16 [3072, 14336], P(('fsdp', 'dp'), 'tenant'), may hold values from -6 to 6
Outputs:
- hidden_out: bfloat16 [3072, 14336], P(('fsdp', 'dp'), 'tenant')
- grad_tokens: bfloat16 [3072, 5120], P(('fsdp', 'dp'), 'tenant')
- grad_down: float32 [8, 64, 5120], P('dp', None, 'tenant')
- grad_up: float32 [8, 64, 14336], P('dp', None, 'tenant')
Inputs may be any that keep to these rules, and one draw needn't show every extreme that they name: `ranks`: multiples of 16; some tenant has rank 64.
All inputs are finite; a program needn't handle non-finite values.
Results may differ from a plain program's by a relative error of at most 0.0034.
Values may be sent and summed in bfloat16 or wider, within the bound.
A program may use at most 128 MiB of HBM per device.

v0:
```python
import jax
import jax.numpy as jnp
from jax import lax
from jax.sharding import PartitionSpec as P

BLOCK = 64
alpha_scale = 32.0
BF16 = jnp.bfloat16
F32 = jnp.float32


def nt(a, b):
    return lax.dot_general(a, b, (((1,), (1,)), ((), ())), preferred_element_type=F32)


def tn(a, b):
    return lax.dot_general(a, b, (((0,), (0,)), ((), ())), preferred_element_type=F32)


def fetch_adapter(adapter, tenant_n, dp_n):
    share = adapter.shape[1] // dp_n
    mine = lax.dynamic_slice_in_dim(adapter, lax.axis_index("dp") * share, share, axis=1)
    part = lax.all_to_all(mine, "tenant", split_axis=2, concat_axis=0, tiled=True)
    return lax.all_gather(part, "dp", axis=1, tiled=True)


def reduce_fsdp(x, fsdp_n):
    rows = x.shape[0]
    got = lax.all_to_all(
        x.astype(BF16).reshape(fsdp_n, rows // fsdp_n, x.shape[1]), "fsdp", 0, 0, tiled=True
    )
    total = jnp.sum(got.astype(F32), axis=0).astype(BF16)
    return lax.all_gather(total, "fsdp", axis=0, tiled=True).astype(F32)


def make_shards(mesh):
    tenant_n, fsdp_n, dp_n = (mesh.shape["tenant"], mesh.shape["fsdp"], mesh.shape["dp"])

    def shards(
        tokens,
        block_tenant_index,
        ranks,
        frozen_up_weight,
        tenant_down_adapters,
        tenant_up_adapters,
        cotangent,
    ):
        rows, local_d = tokens.shape
        local_f = cotangent.shape[1]
        tenants = ranks.shape[0]
        rank = tenant_down_adapters.shape[1]
        depth = frozen_up_weight.shape[0]
        blocks = fsdp_n * dp_n
        first = max(128, depth * 3 // 5 // 128 * 128) if depth > 128 else depth
        cuts = [(0, first)] + ([(first, depth)] if first < depth else [])
        weights = [
            lax.all_gather(frozen_up_weight[a:b], ("fsdp", "dp"), axis=0, tiled=True)
            for a, b in cuts
        ]
        up = fetch_adapter(tenant_up_adapters, tenant_n, dp_n).reshape(tenants * rank, local_f)
        down = fetch_adapter(tenant_down_adapters, tenant_n, dp_n).reshape(tenants * rank, local_d)
        onehot = block_tenant_index[:, None] == jnp.arange(tenants, dtype=jnp.int32)[None, :]
        sel = onehot.astype(F32)[:, None, :, None]
        own_rank = jnp.sum(jnp.where(onehot, ranks[None, :], 0), axis=1)
        keep = jnp.arange(rank, dtype=jnp.int32)[None, :] < own_rank[:, None]
        gain = jnp.where(keep, (alpha_scale / own_rank.astype(F32))[:, None], F32(0.0))

        def compact(full):
            full = full.reshape(rows // BLOCK, BLOCK, tenants, rank)
            return jnp.sum(full * sel, axis=2)

        both = jnp.concatenate([compact(nt(tokens, down)), compact(nt(cotangent, up))], axis=2)
        both = lax.psum(both, "tenant")

        def spread(values):
            scaled = (values * gain[:, None, :]).astype(BF16)
            return (scaled[:, :, None, :] * sel.astype(BF16)).reshape(rows, tenants * rank)

        adapted = spread(both[:, :, :rank])
        adapted_grad = spread(both[:, :, rank:])
        terms = jnp.concatenate([tn(adapted, cotangent), tn(adapted_grad, tokens)], axis=1)
        terms = lax.psum_scatter(terms, "dp", scatter_dimension=0, tiled=True)
        grads = reduce_fsdp(terms, fsdp_n)
        grad_up = grads[:, :local_f].reshape(tenants // dp_n, rank, local_f)
        grad_down = grads[:, local_f:].reshape(tenants // dp_n, rank, local_d)
        whole = lax.all_gather(tokens, "tenant", axis=1, tiled=True)
        whole3 = whole.reshape(rows, blocks, depth)
        hidden = jnp.dot(adapted, up, preferred_element_type=F32)
        pieces = []
        for (a, b), weight in zip(cuts, weights):
            back = nt(cotangent, weight).astype(BF16)
            n = b - a
            got = lax.all_to_all(
                back.reshape(rows, tenant_n, blocks * n // tenant_n).transpose(1, 0, 2),
                "tenant",
                0,
                0,
                tiled=True,
            )
            pieces.append(jnp.sum(got.astype(F32), axis=0).reshape(rows, blocks // tenant_n, n))
            hidden = hidden + jnp.dot(
                whole3[:, :, a:b].reshape(rows, blocks * n), weight, preferred_element_type=F32
            )
        hidden_out = hidden.astype(BF16)
        grad_base = jnp.concatenate(pieces, axis=2).reshape(rows, local_d)
        grad_tokens = (grad_base + jnp.dot(adapted_grad, down, preferred_element_type=F32)).astype(
            BF16
        )
        return (hidden_out, grad_tokens, grad_down, grad_up)

    return shards


def solution(mesh):
    return jax.shard_map(
        make_shards(mesh),
        mesh=mesh,
        in_specs=(
            P(("fsdp", "dp"), "tenant"),
            P(("fsdp", "dp")),
            P(),
            P(("fsdp", "dp"), "tenant"),
            P("tenant", None, None),
            P("tenant", None, None),
            P(("fsdp", "dp"), "tenant"),
        ),
        out_specs=(
            P(("fsdp", "dp"), "tenant"),
            P(("fsdp", "dp"), "tenant"),
            P("dp", None, "tenant"),
            P("dp", None, "tenant"),
        ),
        check_vma=False,
    )
```

profile of v0, /device:TPU:0, one launch (start us, length us, event | category | flops | bytes accessed | tf_op | source)
XLA Modules:
  0.0 595.5 jit_solution(8852192433115120866)
XLA Ops:
  12.5 4.9 reshape.171
  17.4 6.3 %all-to-all-start = ((bf16[4,2,40960]{2,1,0:T(2,128)(2,1)}), bf16[4,2,40960]{2,1,0:T(2,128)(2,1)S(1)}, u32[]{:S(2)}, u32[]{:S(2)}) async-start(bf16[4,2,40960]{2,1,0:T(2,128)(2,1)} %reshape.171), calls=%async_computation | async-start | bytes 1310720 | tf_op jit(solution)/shard_map/all_to_all | solution.py:23
  26.6 15.2 %copy.31 = bf16[2,32,14336]{1,0,2:T(2,128)(2,1)} copy(bf16[2,32,14336]{2,1,0:T(8,128)(2,1)} %constant_dynamic-slice_fusion) | data formatting | bytes 3670016
  41.9 9.4 %reshape.173 = bf16[4,2,114688]{2,1,0:T(2,128)(2,1)} reshape(bf16[14336,2,32]{2,1,0:T(2,128)(2,1)} %bitcast.65) | data formatting | bytes 3670016
  51.3 5.1 all-to-all-start.1
  59.0 6.2 %copy.28 = bf16[2,32,4,1280]{3,2,1,0:T(4,128)(2,1)S(1)} copy(bf16[2,32,4,1280]{1,0,3,2:T(2,128)(2,1)} %bitcast.70) | data formatting | bytes 1310720 | tf_op jit(solution)/shard_map/all_to_all | solution.py:23
  66.2 32.3 %all-to-all-done.1 = bf16[4,2,114688]{2,1,0:T(2,128)(2,1)} async-done(((bf16[4,2,114688]{2,1,0:T(2,128)(2,1)}), bf16[4,2,114688]{2,1,0:T(2,128)(2,1)}, u32[]{:S(2)}, u32[]{:S(2)}) %all-to-all-start.1) | async-done | bytes 1835040 | tf_op jit(solution)/shard_map/all_to_all | solution.py:23
  98.5 6.9 %reshape.174 = bf16[14336,2,32]{2,1,0:T(2,128)(2,1)} reshape(bf16[4,2,114688]{2,1,0:T(2,128)(2,1)} %all-to-all-done.1) | data formatting | bytes 3670016
  105.4 18.1 %copy.29 = bf16[2,32,4,3584]{3,2,1,0:T(4,128)(2,1)} copy(bf16[2,32,4,3584]{1,0,3,2:T(2,128)(2,1)} %bitcast.66) | data formatting | bytes 3670016 | tf_op jit(solution)/shard_map/all_to_all | solution.py:23
  132.9 5.8 all-gather.9.cloned.1.call-done
  138.7 5.0 convolution_bitcast_fusion
  151.4 35.2 %all-reduce.2.cloned.1.call-done = f32[6,64,128]{2,1,0:T(8,128)} async-done(((f32[6,64,128]{2,1,0:T(8,128)}), f32[6,64,128]{2,1,0:T(8,128)}) %all-reduce.2.cloned.1.call-update) | async-done | bytes 196624 | tf_op jit(solution)/shard_map/psum | solution.py:73
  196.3 5.0 fusion.10
  201.3 8.3 %pad_maximum_fusion = f32[512,4864]{1,0:T(8,128)} fusion(f32[512,1280]{1,0:T(8,128)} %fusion.11, f32[512,3584]{1,0:T(8,128)} %fusion.10), kind=kLoop, calls=%fused_computation | loop fusion | flops 2490368 | bytes 19922944 | tf_op jit(solution)/shard_map/concatenate | solution.py:81
  216.2 48.0 %all-gather.11.cloned.1.call-done = bf16[384,5120]{1,0:T(8,128)(2,1)} async-done(((bf16[384,1280]{1,0:T(8,128)(2,1)}), bf16[384,5120]{1,0:T(8,128)(2,1)}) %all-gather.11.cloned.1.call-update) | async-done | bytes 3932176 | tf_op jit(solution)/shard_map/all_gather | solution.py:86
  271.1 11.4 %reduce-scatter.2.cloned.1.call-done = f32[256,4864]{1,0:T(8,128)} async-done(((f32[512,4864]{1,0:T(8,128)}), f32[256,4864]{1,0:T(8,128)}) %reduce-scatter.2.cloned.1.call-update) | async-done | bytes 4980752 | tf_op jit(solution)/shard_map/reduce_scatter | solution.py:82
  291.2 6.6 %fusion.8 = f32[384,3584]{1,0:T(8,128)} fusion(bf16[384,512]{1,0:T(8,128)(2,1)S(1)} %mul.87, bf16[512,3584]{1,0:T(8,128)(2,1)} %bitcast.82), kind=kOutput, calls=%fused_computation.33 | convolution fusion | flops 1409286144 | bytes 9568256 | tf_op jit(solution)/shard_map/dot_general | solution.py:88
  297.8 92.3 %all-gather.15.cloned.1.call-done = bf16[2048,3584]{1,0:T(8,128)(2,1)} async-done(((bf16[256,3584]{1,0:T(8,128)(2,1)}), bf16[2048,3584]{1,0:T(8,128)(2,1)}) %all-gather.15.cloned.1.call-update) | async-done | bytes 14680080 | tf_op jit(solution)/shard_map/all_gather | solution.py:57
  390.1 9.4 %convolution_convert_fusion.1 = bf16[384,2048]{1,0:T(8,128)(2,1)S(1)} fusion(bf16[384,3584]{1,0:T(8,128)(2,1)S(1)} %copy-done, bf16[2048,3584]{1,0:T(8,128)(2,1)} %all-gather.15.cloned.1.call-done), kind=kOutput, calls=%fused_computation.9 | convolution fusion | flops 5637931008 | bytes 19005440 | tf_op jit(solution)/shard_map/dot_general | solution.py:13
  408.6 95.9 %all-gather.13.cloned.1.call-done = bf16[3072,3584]{1,0:T(8,128)(2,1)} async-done(((bf16[384,3584]{1,0:T(8,128)(2,1)}), bf16[3072,3584]{1,0:T(8,128)(2,1)}) %all-gather.13.cloned.1.call-update) | async-done | bytes 22020112 | tf_op jit(solution)/shard_map/all_gather | solution.py:57
  504.5 14.0 %convolution_convert_fusion = bf16[384,3072]{1,0:T(8,128)(2,1)} fusion(bf16[384,3584]{1,0:T(8,128)(2,1)S(1)} %copy-done, bf16[3072,3584]{1,0:T(8,128)(2,1)} %all-gather.13.cloned.1.call-done), kind=kOutput, calls=%fused_computation.5 | convolution fusion | flops 8456896512 | bytes 27131904 | tf_op jit(solution)/shard_map/dot_general | solution.py:13
  526.5 11.6 %fusion.9 = f32[384,3584]{1,0:T(8,128)} fusion(bf16[384,2048]{1,0:T(8,128)(2,1)S(1)} %bitcast.87, bf16[2048,3584]{1,0:T(8,128)(2,1)} %all-gather.15.cloned.1.call-done), kind=kOutput, calls=%fused_computation.34 | convolution fusion | flops 5637144576 | bytes 21757952 | tf_op jit(solution)/shard_map/dot_general | solution.py:101
  550.1 18.7 %fusion.1 = bf16[384,3584]{1,0:T(8,128)(2,1)} fusion(f32[384,3584]{1,0:T(8,128)} %fusion.9, f32[384,3584]{1,0:T(8,128)} %fusion.8, bf16[384,3072]{1,0:T(8,128)(2,1)S(1)} %bitcast.85, bf16[3072,3584]{1,0:T(8,128)(2,1)} %all-gather.13.cloned.1.call-done), kind=kOutput, calls=%fused_computation.3 | convolution fusion | flops 8459845632 | bytes 38141952 | tf_op jit(solution)/shard_map/dot_general | solution.py:101
  568.8 12.2 %all-to-all-done.2 = bf16[4,384,768]{2,1,0:T(8,128)(2,1)} async-done(((bf16[4,384,768]{2,1,0:T(8,128)(2,1)}), bf16[4,384,768]{2,1,0:T(8,128)(2,1)}, u32[]{:S(2)}, u32[]{:S(2)}) %all-to-all-start.2) | async-done | bytes 2359328 | tf_op jit(solution)/shard_map/all_to_all | solution.py:93
  (82 shorter events, 97.1 us)
Async XLA Ops:
  7.2 131.6 %copy-start = (bf16[384,3584]{1,0:T(8,128)(2,1)S(1)}, bf16[384,3584]{1,0:T(8,128)(2,1)}, u32[]{:S(2)}) copy-start(bf16[384,3584]{1,0:T(8,128)(2,1)} %param.13) | copy-start | bytes 8257540
  17.4 33.8 %all-to-all-start = ((bf16[4,2,40960]{2,1,0:T(2,128)(2,1)}), bf16[4,2,40960]{2,1,0:T(2,128)(2,1)S(1)}, u32[]{:S(2)}, u32[]{:S(2)}) async-start(bf16[4,2,40960]{2,1,0:T(2,128)(2,1)} %reshape.171), calls=%async_computation | async-start | bytes 1310720 | tf_op jit(solution)/shard_map/all_to_all | solution.py:23
  51.3 47.2 %all-to-all-start.1 = ((bf16[4,2,114688]{2,1,0:T(2,128)(2,1)}), bf16[4,2,114688]{2,1,0:T(2,128)(2,1)}, u32[]{:S(2)}, u32[]{:S(2)}) async-start(bf16[4,2,114688]{2,1,0:T(2,128)(2,1)} %reshape.173), calls=%async_computation.1 | async-start | bytes 3670016 | tf_op jit(solution)/shard_map/all_to_all | solution.py:23
  56.4 70.4 %all-gather.7.cloned.1.call-start = ((), (), s32[]{:S(2)}) async-start(), calls=%async_computation.6 | async-start | bytes 1966080 | tf_op jit(solution)/shard_map/all_gather | solution.py:24
  66.1 72.6 %all-gather.9.cloned.1.call-start = ((), (), s32[]{:S(2)}) async-start(), calls=%async_computation.7 | async-start | bytes 5505024 | tf_op jit(solution)/shard_map/all_gather | solution.py:24
  123.5 3.1 copy-start.6
  126.6 60.1 %all-reduce.2.cloned.1.call-start = ((), (), s32[]{:S(2)}) async-start(), calls=%async_computation.8 | async-start | bytes 393216 | tf_op jit(solution)/shard_map/psum | solution.py:73
  146.6 4.6 copy-start.7
  150.3 113.9 %all-gather.11.cloned.1.call-start = ((), (), s32[]{:S(2)}) async-start(), calls=%async_computation.9 | async-start | bytes 4915200 | tf_op jit(solution)/shard_map/all_gather | solution.py:86
  150.9 131.6 %reduce-scatter.2.cloned.1.call-start = ((), (), s32[]{:S(2)}) async-start(), calls=%async_computation.12 | async-start | bytes 14942208 | tf_op jit(solution)/shard_map/reduce_scatter | solution.py:82
  209.6 180.5 %all-gather.15.cloned.1.call-start = ((), (), s32[]{:S(2)}) async-start(), calls=%async_computation.11 | async-start | bytes 16515072 | tf_op jit(solution)/shard_map/all_gather | solution.py:57
  212.6 291.9 %all-gather.13.cloned.1.call-start = ((), (), s32[]{:S(2)}) async-start(), calls=%async_computation.10 | async-start | bytes 24772608 | tf_op jit(solution)/shard_map/all_gather | solution.py:57
  286.6 114.2 %all-to-all-start.4 = ((bf16[4,64,4864]{2,1,0:T(8,128)(2,1)}), bf16[4,64,4864]{2,1,0:T(8,128)(2,1)}, u32[]{:S(2)}, u32[]{:S(2)}) async-start(bf16[4,64,4864]{2,1,0:T(8,128)(2,1)} %bitcast.71), calls=%async_computation.5 | async-start | bytes 4980736 | tf_op jit(solution)/shard_map/all_to_all | solution.py:29
  400.9 120.9 %all-to-all-start.3 = ((bf16[4,384,512]{2,1,0:T(8,128)(2,1)}), bf16[4,384,512]{2,1,0:T(8,128)(2,1)}, u32[]{:S(2)}, u32[]{:S(2)}) async-start(bf16[4,384,512]{2,1,0:T(8,128)(2,1)} %bitcast.77), calls=%async_computation.3 | async-start | bytes 3145728 | tf_op jit(solution)/shard_map/all_to_all | solution.py:93
  405.5 139.9 %all-gather.17.cloned.1.call-start = ((), (), s32[]{:S(2)}) async-start(), calls=%async_computation.13 | async-start | bytes 3112960 | tf_op jit(solution)/shard_map/all_gather | solution.py:33
  521.8 4.7 copy-start.4
  521.8 59.2 %all-to-all-start.2 = ((bf16[4,384,768]{2,1,0:T(8,128)(2,1)}), bf16[4,384,768]{2,1,0:T(8,128)(2,1)}, u32[]{:S(2)}, u32[]{:S(2)}) async-start(bf16[4,384,768]{2,1,0:T(8,128)(2,1)} %bitcast.62), calls=%async_computation.2 | async-start | bytes 4718592 | tf_op jit(solution)/shard_map/all_to_all | solution.py:93
  545.4 2.4 copy-start.2
  547.8 2.3 copy-start.3
  585.8 1.3 copy-start.5
  585.8 2.9 copy-start.1
Sparse Core Ops, SparseCore 0:
  66.2 10.8 all-gather.6
  126.7 11.9 all-gather.8
  150.5 36.1 all-reduce.1
  188.1 76.0 all-gather.10
  266.4 16.1 reduce-scatter.1
  284.3 105.8 all-gather.14
  392.6 111.8 all-gather.12
  506.9 38.4 all-gather.16
where the time goes:
time: 598 us; the launch traced here: 596 us
  waiting for transfers between devices  338 us (57%)
  local copies, waits for them, and re-layouts  111 us (19%)
  matrix products  79 us (13%)
  other arithmetic  27.8 us (5%)
  starting transfers between devices  25.8 us (4%)
  between operations  14.3 us (2%)
    all_gather x2, waiting for transfers between devices, shards(): lax.all_gather(frozen_up_weight[a:b], ('fsdp', 'dp'), axis=0, tiled=True)  188 us
    unnamed x26, local copies, waits for them, and re-layouts  51 us
    all_gather x1, waiting for transfers between devices, shards(): whole = lax.all_gather(tokens, 'tenant', axis=1, tiled=True)  48 us
    psum x1, waiting for transfers between devices, shards(): both = lax.psum(both, 'tenant')  35.2 us
    all_to_all x2, waiting for transfers between devices, fetch_adapter(): lax.all_to_all(mine, 'tenant', split_axis=2, concat_axis=0, tiled=True)  32.3 us
    dot_general x4, matrix products, nt(): lax.dot_general(a, b, (((1,), (1,)), ((), ())), preferred_element_type=F32)  31.8 us
    dot_general x2, matrix products, shards(): jnp.dot(whole3[:, :, a:b].reshape(rows, blocks * n), weight, preferred_el...  30.3 us
    all_to_all x4, local copies, waits for them, and re-layouts, fetch_adapter(): lax.all_to_all(mine, 'tenant', split_axis=2, concat_axis=0, tiled=True)  28.3 us
  transfers between devices with their start and end apart: 13, of which 9 were waited for; matrix products, arithmetic and copies ran while one was open for 32% of the time, Pallas kernels for 0%

commit v1 on v0

--- a/solution.py
+++ b/solution.py
@@ -20,7 +20,10 @@
 def fetch_adapter(adapter, tenant_n, dp_n):
     share = adapter.shape[1] // dp_n
     mine = lax.dynamic_slice_in_dim(adapter, lax.axis_index("dp") * share, share, axis=1)
-    part = lax.all_to_all(mine, "tenant", split_axis=2, concat_axis=0, tiled=True)
+    part = jnp.concatenate(
+        lax.all_to_all(jnp.stack(jnp.split(mine, lax.axis_size("tenant"), axis=2)), "tenant", 0, 0),
+        axis=0,
+    )
     return lax.all_gather(part, "dp", axis=1, tiled=True)
 
 

time: 598 us -> 550 us (0.920)
  local copies, waits for them, and re-layouts: 111 us -> 38 us
  waiting for transfers between devices: 338 us -> 362 us
    unnamed x26 -> x22, local copies, waits for them, and re-layouts: 51 us -> 7.95 us
    all_to_all x4 -> x0, local copies, waits for them, and re-layouts: 28.3 us -> none  [fetch_adapter(): lax.all_to_all(mine, 'tenant', split_axis=2, concat_axis=0, tiled=True)]
    all_to_all x2, waiting for transfers between devices: 32.3 us -> 55.7 us  [fetch_adapter(): lax.all_to_all(jnp.stack(jnp.split(mine, lax.axis_size('tenant'), axis=2)...]
  transfers between devices with their start and end apart: 13 -> 13, of which waited for: 9 -> 10; matrix products, arithmetic and copies ran while one was open for 32% -> 23% of each run, Pallas kernels for 0% -> 0%
where the time goes in v1:
time: 550 us; the launch traced here: 549 us
  waiting for transfers between devices  362 us (66%)
  matrix products  79 us (14%)
  local copies, waits for them, and re-layouts  38 us (7%)
  other arithmetic  30.2 us (5%)
  starting transfers between devices  25.2 us (5%)
  between operations  14.3 us (3%)
    all_gather x2, waiting for transfers between devices, shards(): lax.all_gather(frozen_up_weight[a:b], ('fsdp', 'dp'), axis=0, tiled=True)  188 us
    all_to_all x2, waiting for transfers between devices, fetch_adapter(): lax.all_to_all(jnp.stack(jnp.split(mine, lax.axis_size('tenant'), axis=2)...  55.7 us
    all_gather x1, waiting for transfers between devices, shards(): whole = lax.all_gather(tokens, 'tenant', axis=1, tiled=True)  47.8 us
    psum x1, waiting for transfers between devices, shards(): both = lax.psum(both, 'tenant')  35.4 us
    dot_general x4, matrix products, nt(): lax.dot_general(a, b, (((1,), (1,)), ((), ())), preferred_element_type=F32)  31.8 us
    dot_general x2, matrix products, shards(): jnp.dot(whole3[:, :, a:b].reshape(rows, blocks * n), weight, preferred_el...  30.3 us
    all_to_all x2, waiting for transfers between devices, shards(): lax.all_to_all(back.reshape(rows, tenant_n, blocks * n // tenant_n).trans...  12.2 us
    reduce_scatter x1, waiting for transfers between devices, shards(): terms = lax.psum_scatter(terms, 'dp', scatter_dimension=0, tiled=True)  11.4 us
  transfers between devices with their start and end apart: 13, of which 10 were waited for; matrix products, arithmetic and copies ran while one was open for 23% of the time, Pallas kernels for 0%

profile of v1, /device:TPU:0, one launch (start us, length us, event | category | flops | bytes accessed | tf_op | source)
XLA Modules:
  0.0 548.7 jit_solution(15787968671821705637)
XLA Ops:
  9.5 6.3 %all-to-all-start = ((bf16[4,2,32,1280]{3,2,1,0:T(8,128)(2,1)}), bf16[4,2,32,1280]{3,2,1,0:T(8,128)(2,1)S(1)}, u32[]{:S(2)}, u32[]{:S(2)}) async-start(bf16[4,2,32,1280]{3,2,1,0:T(8,128)(2,1)} %pad_maximum_fusion.3), calls=%async_computation | async-start | bytes 1310720 | tf_op jit(solution)/shard_map/all_to_all | solution.py:24
  18.9 14.2 %all-to-all-done = bf16[4,2,32,1280]{3,2,1,0:T(8,128)(2,1)S(1)} async-done(((bf16[4,2,32,1280]{3,2,1,0:T(8,128)(2,1)}), bf16[4,2,32,1280]{3,2,1,0:T(8,128)(2,1)S(1)}, u32[]{:S(2)}, u32[]{:S(2)}) %all-to-all-start) | async-done | bytes 655392 | tf_op jit(solution)/shard_map/all_to_all | solution.py:24
  33.1 4.4 all-to-all-start.1
  38.3 41.4 %all-to-all-done.1 = bf16[4,2,32,3584]{3,2,1,0:T(8,128)(2,1)} async-done(((bf16[4,2,32,3584]{3,2,1,0:T(8,128)(2,1)}), bf16[4,2,32,3584]{3,2,1,0:T(8,128)(2,1)}, u32[]{:S(2)}, u32[]{:S(2)}) %all-to-all-start.1) | async-done | bytes 1835040 | tf_op jit(solution)/shard_map/all_to_all | solution.py:24
  86.1 5.8 %all-gather.9.cloned.1.call-done = bf16[8,64,3584]{2,1,0:T(8,128)(2,1)} async-done(((bf16[8,32,3584]{2,1,0:T(8,128)(2,1)}), bf16[8,64,3584]{2,1,0:T(8,128)(2,1)}) %all-gather.9.cloned.1.call-update) | async-done | bytes 3670032 | tf_op jit(solution)/shard_map/all_gather | solution.py:27
  91.9 5.0 convolution_bitcast_fusion
  104.4 35.4 %all-reduce.2.cloned.1.call-done = f32[6,64,128]{2,1,0:T(8,128)} async-done(((f32[6,64,128]{2,1,0:T(8,128)}), f32[6,64,128]{2,1,0:T(8,128)}) %all-reduce.2.cloned.1.call-update) | async-done | bytes 196624 | tf_op jit(solution)/shard_map/psum | solution.py:76
  149.4 5.0 fusion.10
  154.5 8.3 %pad_maximum_fusion = f32[512,4864]{1,0:T(8,128)} fusion(f32[512,1280]{1,0:T(8,128)} %fusion.11, f32[512,3584]{1,0:T(8,128)} %fusion.10), kind=kLoop, calls=%fused_computation | loop fusion | flops 2490368 | bytes 19922944 | tf_op jit(solution)/shard_map/concatenate | solution.py:84
  169.5 47.8 %all-gather.11.cloned.1.call-done = bf16[384,5120]{1,0:T(8,128)(2,1)} async-done(((bf16[384,1280]{1,0:T(8,128)(2,1)}), bf16[384,5120]{1,0:T(8,128)(2,1)}) %all-gather.11.cloned.1.call-update) | async-done | bytes 3932176 | tf_op jit(solution)/shard_map/all_gather | solution.py:89
  224.3 11.4 %reduce-scatter.2.cloned.1.call-done = f32[256,4864]{1,0:T(8,128)} async-done(((f32[512,4864]{1,0:T(8,128)}), f32[256,4864]{1,0:T(8,128)}) %reduce-scatter.2.cloned.1.call-update) | async-done | bytes 4980752 | tf_op jit(solution)/shard_map/reduce_scatter | solution.py:85
  235.7 4.1 convert_element_type.69
  239.8 4.5 all-to-all-start.4
  244.3 6.6 %fusion.8 = f32[384,3584]{1,0:T(8,128)} fusion(bf16[384,512]{1,0:T(8,128)(2,1)S(1)} %mul.87, bf16[512,3584]{1,0:T(8,128)(2,1)} %bitcast.84), kind=kOutput, calls=%fused_computation.41 | convolution fusion | flops 1409286144 | bytes 9568256 | tf_op jit(solution)/shard_map/dot_general | solution.py:91
  251.0 92.3 %all-gather.15.cloned.1.call-done = bf16[2048,3584]{1,0:T(8,128)(2,1)} async-done(((bf16[256,3584]{1,0:T(8,128)(2,1)}), bf16[2048,3584]{1,0:T(8,128)(2,1)}) %all-gather.15.cloned.1.call-update) | async-done | bytes 14680080 | tf_op jit(solution)/shard_map/all_gather | solution.py:60
  343.3 9.4 %convolution_convert_fusion.1 = bf16[384,2048]{1,0:T(8,128)(2,1)S(1)} fusion(bf16[384,3584]{1,0:T(8,128)(2,1)S(1)} %copy-done, bf16[2048,3584]{1,0:T(8,128)(2,1)} %all-gather.15.cloned.1.call-done), kind=kOutput, calls=%fused_computation.9 | convolution fusion | flops 5637931008 | bytes 19005440 | tf_op jit(solution)/shard_map/dot_general | solution.py:13
  354.0 4.6 all-to-all-start.3
  361.7 96.0 %all-gather.13.cloned.1.call-done = bf16[3072,3584]{1,0:T(8,128)(2,1)} async-done(((bf16[384,3584]{1,0:T(8,128)(2,1)}), bf16[3072,3584]{1,0:T(8,128)(2,1)}) %all-gather.13.cloned.1.call-update) | async-done | bytes 22020112 | tf_op jit(solution)/shard_map/all_gather | solution.py:60
  457.7 14.1 %convolution_convert_fusion = bf16[384,3072]{1,0:T(8,128)(2,1)} fusion(bf16[384,3584]{1,0:T(8,128)(2,1)S(1)} %copy-done, bf16[3072,3584]{1,0:T(8,128)(2,1)} %all-gather.13.cloned.1.call-done), kind=kOutput, calls=%fused_computation.5 | convolution fusion | flops 8456896512 | bytes 27131904 | tf_op jit(solution)/shard_map/dot_general | solution.py:13
  474.9 4.9 all-to-all-start.2
  479.8 11.6 %fusion.9 = f32[384,3584]{1,0:T(8,128)} fusion(bf16[384,2048]{1,0:T(8,128)(2,1)S(1)} %bitcast.88, bf16[2048,3584]{1,0:T(8,128)(2,1)} %all-gather.15.cloned.1.call-done), kind=kOutput, calls=%fused_computation.42 | convolution fusion | flops 5637144576 | bytes 21757952 | tf_op jit(solution)/shard_map/dot_general | solution.py:104
  494.5 4.0 all-gather.17.cloned.1.call-done
  503.2 18.7 %fusion.1 = bf16[384,3584]{1,0:T(8,128)(2,1)} fusion(f32[384,3584]{1,0:T(8,128)} %fusion.9, f32[384,3584]{1,0:T(8,128)} %fusion.8, bf16[384,3072]{1,0:T(8,128)(2,1)S(1)} %bitcast.86, bf16[3072,3584]{1,0:T(8,128)(2,1)} %all-gather.13.cloned.1.call-done), kind=kOutput, calls=%fused_computation.3 | convolution fusion | flops 8459845632 | bytes 38141952 | tf_op jit(solution)/shard_map/dot_general | solution.py:104
  522.0 12.2 %all-to-all-done.2 = bf16[4,384,768]{2,1,0:T(8,128)(2,1)} async-done(((bf16[4,384,768]{2,1,0:T(8,128)(2,1)}), bf16[4,384,768]{2,1,0:T(8,128)(2,1)}, u32[]{:S(2)}, u32[]{:S(2)}) %all-to-all-start.2) | async-done | bytes 2359328 | tf_op jit(solution)/shard_map/all_to_all | solution.py:96
  (76 shorter events, 66.1 us)
Async XLA Ops:
  7.2 84.7 %copy-start = (bf16[384,3584]{1,0:T(8,128)(2,1)S(1)}, bf16[384,3584]{1,0:T(8,128)(2,1)}, u32[]{:S(2)}) copy-start(bf16[384,3584]{1,0:T(8,128)(2,1)} %param.13) | copy-start | bytes 8257540
  9.5 23.6 %all-to-all-start = ((bf16[4,2,32,1280]{3,2,1,0:T(8,128)(2,1)}), bf16[4,2,32,1280]{3,2,1,0:T(8,128)(2,1)S(1)}, u32[]{:S(2)}, u32[]{:S(2)}) async-start(bf16[4,2,32,1280]{3,2,1,0:T(8,128)(2,1)} %pad_maximum_fusion.3), calls=%async_computation | async-start | bytes 1310720 | tf_op jit(solution)/shard_map/all_to_all | solution.py:24
  18.9 60.9 %copy-start.7 = (s32[6]{0:T(128)S(1)}, s32[6]{0:T(128)}, u32[]{:S(2)}) copy-start(s32[6]{0:T(128)} %param.8) | copy-start | bytes 76
  33.1 4.5 copy-start.3
  33.1 46.6 %all-to-all-start.1 = ((bf16[4,2,32,3584]{3,2,1,0:T(8,128)(2,1)}), bf16[4,2,32,3584]{3,2,1,0:T(8,128)(2,1)}, u32[]{:S(2)}, u32[]{:S(2)}) async-start(bf16[4,2,32,3584]{3,2,1,0:T(8,128)(2,1)} %pad_maximum_fusion.2), calls=%async_computation.1 | async-start | bytes 3670016 | tf_op jit(solution)/shard_map/all_to_all | solution.py:24
  37.5 42.4 %all-gather.7.cloned.1.call-start = ((), (), s32[]{:S(2)}) async-start(), calls=%async_computation.6 | async-start | bytes 1966080 | tf_op jit(solution)/shard_map/all_gather | solution.py:27
  38.3 53.6 %all-gather.9.cloned.1.call-start = ((), (), s32[]{:S(2)}) async-start(), calls=%async_computation.7 | async-start | bytes 5505024 | tf_op jit(solution)/shard_map/all_gather | solution.py:27
  79.8 60.1 %all-reduce.2.cloned.1.call-start = ((), (), s32[]{:S(2)}) async-start(), calls=%async_computation.8 | async-start | bytes 393216 | tf_op jit(solution)/shard_map/psum | solution.py:76
  99.8 4.4 copy-start.8
  103.5 113.9 %all-gather.11.cloned.1.call-start = ((), (), s32[]{:S(2)}) async-start(), calls=%async_computation.9 | async-start | bytes 4915200 | tf_op jit(solution)/shard_map/all_gather | solution.py:89
  104.1 131.6 %reduce-scatter.2.cloned.1.call-start = ((), (), s32[]{:S(2)}) async-start(), calls=%async_computation.12 | async-start | bytes 14942208 | tf_op jit(solution)/shard_map/reduce_scatter | solution.py:85
  162.8 180.5 %all-gather.15.cloned.1.call-start = ((), (), s32[]{:S(2)}) async-start(), calls=%async_computation.11 | async-start | bytes 16515072 | tf_op jit(solution)/shard_map/all_gather | solution.py:60
  165.8 291.9 %all-gather.13.cloned.1.call-start = ((), (), s32[]{:S(2)}) async-start(), calls=%async_computation.10 | async-start | bytes 24772608 | tf_op jit(solution)/shard_map/all_gather | solution.py:60
  239.8 114.2 %all-to-all-start.4 = ((bf16[4,64,4864]{2,1,0:T(8,128)(2,1)}), bf16[4,64,4864]{2,1,0:T(8,128)(2,1)}, u32[]{:S(2)}, u32[]{:S(2)}) async-start(bf16[4,64,4864]{2,1,0:T(8,128)(2,1)} %bitcast.75), calls=%async_computation.5 | async-start | bytes 4980736 | tf_op jit(solution)/shard_map/all_to_all | solution.py:32
  354.0 120.9 %all-to-all-start.3 = ((bf16[4,384,512]{2,1,0:T(8,128)(2,1)}), bf16[4,384,512]{2,1,0:T(8,128)(2,1)}, u32[]{:S(2)}, u32[]{:S(2)}) async-start(bf16[4,384,512]{2,1,0:T(8,128)(2,1)} %bitcast.79), calls=%async_computation.3 | async-start | bytes 3145728 | tf_op jit(solution)/shard_map/all_to_all | solution.py:96
  358.6 139.9 %all-gather.17.cloned.1.call-start = ((), (), s32[]{:S(2)}) async-start(), calls=%async_computation.13 | async-start | bytes 3112960 | tf_op jit(solution)/shard_map/all_gather | solution.py:36
  474.9 4.9 copy-start.5
  474.9 59.3 %all-to-all-start.2 = ((bf16[4,384,768]{2,1,0:T(8,128)(2,1)}), bf16[4,384,768]{2,1,0:T(8,128)(2,1)}, u32[]{:S(2)}, u32[]{:S(2)}) async-start(bf16[4,384,768]{2,1,0:T(8,128)(2,1)} %bitcast.70), calls=%async_computation.2 | async-start | bytes 4718592 | tf_op jit(solution)/shard_map/all_to_all | solution.py:96
  498.5 2.4 copy-start.2
  500.9 2.3 copy-start.4
  538.9 1.3 copy-start.6
  538.9 2.9 copy-start.1
Sparse Core Ops, SparseCore 0:
  40.5 10.8 all-gather.6
  79.9 11.9 all-gather.8
  103.6 36.1 all-reduce.1
  141.3 76.0 all-gather.10
  219.5 16.1 reduce-scatter.1
  237.4 105.7 all-gather.14
  345.7 111.8 all-gather.12
  460.1 38.4 all-gather.16
